TPU v7x, 128 devices: a whole 4x4x4 slice. The times are simulated.
128 devices in a mesh: dp: 8 (over y, core), pipe: 4 (over x), tensor: 4 (over z).
Axes of the slice: x: 4, y: 4, z: 4, core: 2. Of those that a mesh axis runs over, the one named last changes fastest.
Arguments:
- query_states: bfloat16 [16, 512, 1024], P('dp'), may hold values from -6 to 6
- doc_states: bfloat16 [16, 512, 1024], P('dp'), may hold values from -6 to 6
- query_len: int32 [16], P('dp'), may hold values from 64 to 512
- doc_len: int32 [16], P('dp'), may hold values from 64 to 512
- doc_order: int32 [8, 2], P('dp'), may hold values from 0 to 1, each once within a row
- w_qkv: bfloat16 [4, 3, 1024, 1024], P('pipe', None, None, 'tensor'), may hold values from -0.1875 to 0.1875
- w_out: bfloat16 [4, 1024, 1024], P('pipe', 'tensor'), may hold values from -0.1875 to 0.1875
- w_up: bfloat16 [4, 1024, 4096], P('pipe', None, 'tensor'), may hold values from -0.1875 to 0.1875
- w_down: bfloat16 [4, 4096, 1024], P('pipe', 'tensor'), may hold values from -0.09375 to 0.09375
- gain_attn: float32 [4, 1024], P('pipe'), may hold values from 0.1 to 1.9
- gain_mlp: float32 [4, 1024], P('pipe'), may hold values from 0.1 to 1.9
Outputs:
- query_vectors: bfloat16 [16, 1024], P('dp', ('pipe', 'tensor'))
- document_vectors: bfloat16 [16, 1024], P('dp', ('pipe', 'tensor'))
- pair_loss: float32 [16], P('dp')
Inputs may be any that keep to these rules, and one draw needn't show every extreme that they name: `doc_order`: each row holds every number of 0 to 1 once.
All inputs are finite; a program needn't handle non-finite values.
Results may differ from a plain program's by a relative error of at most 0.035.
Values may be sent and summed in bfloat16 or wider, within the bound.
A program may use at most 192 MiB of HBM per device.

v0:
```python
import math
import jax
import jax.numpy as jnp
from jax import lax
from jax.sharding import PartitionSpec as P

D = 1024
HEADS = 16
SOFTMAX_TEMPER = 0.05
EPSILON = 1e-06
LAYER_EPSILON = 1e-12


def from_behind(value, axis, steps):
    count = lax.axis_size(axis)
    initial, last = (max(0, -steps), min(count, count - steps))
    return lax.ppermute(value, axis, [(source, source + steps) for source in range(initial, last)])


def from_root(x, axis, root):
    return lax.dynamic_index_in_dim(lax.all_gather(x, axis), root, 0, keepdims=False)


def laid_out(parts, dim):
    lengths = list(parts.shape[1:])
    lengths[dim] *= parts.shape[0]
    return jnp.moveaxis(parts, 0, dim).reshape(lengths)


def copy_for_each(x, axis):
    peers = lax.axis_size(axis)
    return lax.all_to_all(jnp.broadcast_to(x[None], (peers, *x.shape)), axis, 0, 0, tiled=True)


def collect(x, axis, dim):
    return laid_out(copy_for_each(x, axis), dim)


def of_everyone(x, axis):
    return copy_for_each(x, axis).sum(axis=0)


def norm_rows(values_in, gain_row):
    row_mean = jnp.mean(values_in, axis=-1, keepdims=True)
    centered = values_in - row_mean
    variance = jnp.mean(centered * centered, axis=-1, keepdims=True)
    return centered * lax.rsqrt(variance + LAYER_EPSILON) * gain_row


def local_reduce(left_side, right_side, residual, gain_row, group_count):
    row_total = left_side.shape[0]
    group_width = left_side.shape[1] // group_count
    left_parts = left_side.reshape(row_total, group_count, group_width)
    right_parts = right_side.reshape(group_count, group_width, right_side.shape[1])
    partials = jnp.einsum(
        "sgk,gkd->gsd", left_parts, right_parts, preferred_element_type=jnp.float32
    )
    summed = jnp.sum(partials.astype(jnp.bfloat16).astype(jnp.float32), axis=0)
    return norm_rows(residual.astype(jnp.float32) + summed, gain_row).astype(jnp.bfloat16)


def reduce_block(left_side, right_side, residual, gain_row, group_count):
    return local_reduce(left_side, right_side, residual, gain_row, group_count)


def encode_layer(hidden, valid_keys, w_qkv, w_out, w_up, w_down, gain_attn, gain_mlp, group_count):
    head_width = D // HEADS
    local_width = w_qkv.shape[-1]
    head_count = local_width // head_width
    slot_count = hidden.shape[0]
    inv_sqrt = 1.0 / math.sqrt(head_width)
    query_rows = (jnp.dot(hidden, w_qkv[0], preferred_element_type=jnp.float32) * inv_sqrt).astype(
        jnp.bfloat16
    )
    key_rows = jnp.dot(hidden, w_qkv[1], preferred_element_type=jnp.float32).astype(jnp.bfloat16)
    value_rows = jnp.dot(hidden, w_qkv[2], preferred_element_type=jnp.float32).astype(jnp.bfloat16)
    query_heads = query_rows.reshape(slot_count, head_count, head_width)
    key_heads = key_rows.reshape(slot_count, head_count, head_width)
    value_heads = value_rows.reshape(slot_count, head_count, head_width)
    scores = jnp.einsum("qhe,khe->hqk", query_heads, key_heads, preferred_element_type=jnp.float32)
    exp_scores = jnp.where(valid_keys[None, None, :], jnp.exp(scores), 0.0)
    attention = (exp_scores / jnp.sum(exp_scores, axis=-1, keepdims=True)).astype(jnp.bfloat16)
    context = jnp.einsum("hqk,khe->qhe", attention, value_heads, preferred_element_type=jnp.float32)
    context = context.astype(jnp.bfloat16).reshape(slot_count, local_width)
    mixed = reduce_block(context, w_out, hidden, gain_attn, group_count)
    upward = jnp.dot(mixed, w_up, preferred_element_type=jnp.float32)
    activated = jax.nn.gelu(upward, approximate=False).astype(jnp.bfloat16)
    return reduce_block(activated, w_down, mixed, gain_mlp, group_count)


def interior_rows(left_side, right_side):
    return lax.dot_general(
        left_side, right_side, (((1,), (1,)), ((), ())), preferred_element_type=jnp.float32
    )


def per_device(
    query_states,
    doc_states,
    query_len,
    doc_len,
    doc_order,
    w_qkv,
    w_out,
    w_up,
    w_down,
    gain_attn,
    gain_mlp,
):
    pair_count = query_states.shape[0]
    seq_count = 2 * pair_count
    slot_count = query_states.shape[1]
    model_width = query_states.shape[2]
    section_count = lax.axis_size("pipe")
    section_index = lax.axis_index("pipe")
    tensor_count = lax.axis_size("tensor")
    lengths = jnp.concatenate([query_len, doc_len])
    positions = jnp.arange(slot_count, dtype=jnp.int32)
    piece_width = model_width // (section_count * tensor_count)
    w_qkv, w_out, w_up, w_down = (
        lax.all_gather(w_qkv, "tensor", axis=3, tiled=True),
        lax.all_gather(w_out, "tensor", axis=1, tiled=True),
        lax.all_gather(w_up, "tensor", axis=2, tiled=True),
        lax.all_gather(w_down, "tensor", axis=1, tiled=True),
    )
    share = seq_count // tensor_count
    first_seq = lax.axis_index("tensor") * share
    local_ids = jnp.arange(share, dtype=jnp.int32)

    def tick_step(tick_index, state_pair):
        passed, pooled = state_pair
        entry_index = first_seq + jnp.clip(tick_index, 0, share - 1)
        query_pick = query_states[jnp.minimum(entry_index, pair_count - 1)]
        doc_pick = doc_states[jnp.clip(entry_index - pair_count, 0, pair_count - 1)]
        fresh = jnp.where(entry_index < pair_count, query_pick, doc_pick)
        hidden = jnp.where(section_index == 0, fresh, passed)
        local_index = jnp.clip(tick_index - section_index, 0, share - 1)
        seq_length = lengths[first_seq + local_index]
        valid_keys = positions < seq_length
        hidden = encode_layer(
            hidden,
            valid_keys,
            w_qkv[0],
            w_out[0],
            w_up[0],
            w_down[0],
            gain_attn[0],
            gain_mlp[0],
            tensor_count,
        )
        finished = tick_index - (section_count - 1)
        store_now = (section_index == section_count - 1) & (finished >= 0)
        summed = jnp.sum(jnp.where(valid_keys[:, None], hidden.astype(jnp.float32), 0.0), axis=0)
        mean_row = summed / seq_length.astype(jnp.float32)
        row_mask = (local_ids == local_index) & store_now
        pooled = jnp.where(row_mask[:, None], mean_row[None, :], pooled)
        passed = from_behind(hidden, "pipe", 1)
        return (passed, pooled)

    start_pair = (
        jnp.zeros((slot_count, model_width), jnp.bfloat16),
        jnp.zeros((share, model_width), jnp.float32),
    )
    unused_state, pooled = lax.fori_loop(0, share + section_count - 1, tick_step, start_pair)
    embedded = (
        pooled * lax.rsqrt(jnp.sum(pooled * pooled, axis=1, keepdims=True) + EPSILON)
    ).astype(jnp.bfloat16)
    grouped = embedded.reshape(share, section_count, tensor_count, piece_width)
    moved = lax.all_to_all(grouped, "tensor", split_axis=2, concat_axis=0, tiled=True)
    tensor_cols = moved.reshape(seq_count, section_count, piece_width)
    shared = from_root(tensor_cols, "pipe", section_count - 1)
    own_piece = lax.dynamic_index_in_dim(shared, section_index, 1, keepdims=False)
    query_portion = own_piece[:pair_count]
    document_portion = own_piece[pair_count:]
    order_row = doc_order[0]
    data_count = lax.axis_size("dp")
    partial_table = interior_rows(query_portion, collect(document_portion, "dp", 0))
    score_table = of_everyone(partial_table, ("pipe", "tensor")) / SOFTMAX_TEMPER
    column_ids = jnp.arange(pair_count * data_count, dtype=jnp.int32)
    target = lax.axis_index("dp") * pair_count + order_row
    is_positive = column_ids[None, :] == target[:, None]
    positive_score = jnp.sum(jnp.where(is_positive, score_table, 0.0), axis=1)
    exp_total = jnp.sum(jnp.exp(score_table), axis=1)
    pair_loss = jnp.log(exp_total) - positive_score
    return (query_portion, document_portion, pair_loss)


def solution(mesh):
    in_specs = (
        P("dp", None, None),
        P("dp", None, None),
        P("dp"),
        P("dp"),
        P("dp", None),
        P("pipe", None, None, "tensor"),
        P("pipe", "tensor", None),
        P("pipe", None, "tensor"),
        P("pipe", "tensor", None),
        P("pipe", None),
        P("pipe", None),
    )
    out_specs = (P("dp", ("pipe", "tensor")), P("dp", ("pipe", "tensor")), P("dp"))
    return jax.shard_map(
        per_device, mesh=mesh, in_specs=in_specs, out_specs=out_specs, check_vma=False
    )
```

profile of v0, /device:TPU:0, one launch (start us, length us, event | category | flops | bytes accessed | tf_op | source)
XLA Modules:
  0.0 658.8 jit_solution(12119853464796553148)
XLA Ops:
  10.7 32.4 %all-gather.8.cloned.1.call-done = bf16[1,1024,1024]{2,1,0:T(8,128)(2,1)} async-done(((bf16[1,256,1024]{2,1,0:T(8,128)(2,1)}), bf16[1,1024,1024]{2,1,0:T(8,128)(2,1)}) %all-gather.8.cloned.1.call-update) | async-done | bytes 2097168 | tf_op jit(solution)/shard_map/all_gather | solution.py:122
  43.2 70.9 %all-gather.6.cloned.1.call-done = bf16[1,3,1024,1024]{3,2,1,0:T(8,128)(2,1)} async-done(((bf16[1,3,1024,256]{3,2,1,0:T(8,128)(2,1)}), bf16[1,3,1024,1024]{3,2,1,0:T(8,128)(2,1)}) %all-gather.6.cloned.1.call-update) | async-done | bytes 6291472 | tf_op jit(solution)/shard_map/all_gather | solution.py:121
  114.0 85.5 %all-gather.10.cloned.1.call-done = bf16[1,1024,4096]{2,1,0:T(8,128)(2,1)} async-done(((bf16[1,1024,1024]{2,1,0:T(8,128)(2,1)}), bf16[1,1024,4096]{2,1,0:T(8,128)(2,1)}) %all-gather.10.cloned.1.call-update) | async-done | bytes 8388624 | tf_op jit(solution)/shard_map/all_gather | solution.py:123
  199.5 85.6 %all-gather.12.cloned.1.call-done = bf16[1,4096,1024]{2,1,0:T(8,128)(2,1)} async-done(((bf16[1,1024,1024]{2,1,0:T(8,128)(2,1)}), bf16[1,4096,1024]{2,1,0:T(8,128)(2,1)}) %all-gather.12.cloned.1.call-update) | async-done | bytes 8388624 | tf_op jit(solution)/shard_map/all_gather | solution.py:124
  285.3 318.5 %while.18 = (s32[]{:T(128)}, bf16[512,1024]{1,0:T(8,128)(2,1)S(1)}, f32[1,1024]{1,0:T(1,128)S(1)}, pred[]{:T(512)}, s32[]{:T(128)}, /*index=5*/bf16[2,512,1024]{...) while((s32[]{:T(128)}, bf16[512,1024]{1,0:T(8,128)(2,1)S(1)}, ...), condition=%wide.region_9.10_spmd.clone, body=%wide.region_0.9_spmd.clone.sunk | while | flops 14147382272 | bytes 201497376 | solution.py:164
  285.3 1.8 bitcast_select_fusion.2
  287.2 3.0 multiply_convert_fusion.6
  290.2 2.2 fusion.92
  292.4 2.3 fusion.91
  295.3 1.5 copy.80
  298.1 2.3 copy.78
  300.3 3.8 fusion.93
  304.1 3.1 fusion.94
  307.3 1.3 convert_reduce_fusion.5
  311.0 22.6 %fusion.96 = bf16[512,4096]{1,0:T(8,128)(2,1)S(1)} fusion(bf16[512,1024]{1,0:T(8,128)(2,1)S(1)} %multiply_convert_fusion.7, bf16[1,1024,4096]{2,1,0:T(8,128)(2,1)S(1)} %bitcast.137), kind=kOutput, calls=%fused_computation.7.clone.1 | convolution fusion | flops 4431282176 | bytes 13631488 | tf_op jit(solution)/shard_map/while/body/eval_jaxpr/dot_general | solution.py:86
  333.7 4.9 convert_reduce_fusion.6
  339.9 3.4 collective-permute-start
  344.0 21.5 %collective-permute-done = bf16[512,1024]{1,0:T(8,128)(2,1)S(1)} collective-permute-done((bf16[512,1024]{1,0:T(8,128)(2,1)S(1)}, bf16[512,1024]{1,0:T(8,128)(2,1)S(1)}, u32[]{:S(2)}, u32[]{:S(2)}) %collective-permute-start) | collective-permute-done | bytes 1048608 | tf_op jit(solution)/shard_map/while/body/eval_jaxpr/ppermute | solution.py:17
  365.5 1.8 bitcast_select_fusion.2
  367.3 3.0 multiply_convert_fusion.6
  370.4 2.2 fusion.92
  372.6 2.3 fusion.91
  375.5 1.5 copy.80
  378.2 2.3 copy.78
  380.5 3.8 fusion.93
  384.3 3.1 fusion.94
  387.5 1.3 convert_reduce_fusion.5
  391.2 22.6 %fusion.96 = bf16[512,4096]{1,0:T(8,128)(2,1)S(1)} fusion(bf16[512,1024]{1,0:T(8,128)(2,1)S(1)} %multiply_convert_fusion.7, bf16[1,1024,4096]{2,1,0:T(8,128)(2,1)S(1)} %bitcast.137), kind=kOutput, calls=%fused_computation.7.clone.1 | convolution fusion | flops 4431282176 | bytes 13631488 | tf_op jit(solution)/shard_map/while/body/eval_jaxpr/dot_general | solution.py:86
  413.8 4.9 convert_reduce_fusion.6
  420.0 4.4 collective-permute-start
  425.2 20.6 %collective-permute-done = bf16[512,1024]{1,0:T(8,128)(2,1)S(1)} collective-permute-done((bf16[512,1024]{1,0:T(8,128)(2,1)S(1)}, bf16[512,1024]{1,0:T(8,128)(2,1)S(1)}, u32[]{:S(2)}, u32[]{:S(2)}) %collective-permute-start) | collective-permute-done | bytes 1048608 | tf_op jit(solution)/shard_map/while/body/eval_jaxpr/ppermute | solution.py:17
  445.8 1.8 bitcast_select_fusion.2
  447.6 3.0 multiply_convert_fusion.6
  450.7 2.2 fusion.92
  452.9 2.3 fusion.91
  455.8 1.5 copy.80
  458.5 2.3 copy.78
  460.8 3.8 fusion.93
  464.6 3.1 fusion.94
  467.8 1.3 convert_reduce_fusion.5
  471.5 22.6 %fusion.96 = bf16[512,4096]{1,0:T(8,128)(2,1)S(1)} fusion(bf16[512,1024]{1,0:T(8,128)(2,1)S(1)} %multiply_convert_fusion.7, bf16[1,1024,4096]{2,1,0:T(8,128)(2,1)S(1)} %bitcast.137), kind=kOutput, calls=%fused_computation.7.clone.1 | convolution fusion | flops 4431282176 | bytes 13631488 | tf_op jit(solution)/shard_map/while/body/eval_jaxpr/dot_general | solution.py:86
  494.1 4.9 convert_reduce_fusion.6
  500.3 4.4 collective-permute-start
  505.4 19.8 %collective-permute-done = bf16[512,1024]{1,0:T(8,128)(2,1)S(1)} collective-permute-done((bf16[512,1024]{1,0:T(8,128)(2,1)S(1)}, bf16[512,1024]{1,0:T(8,128)(2,1)S(1)}, u32[]{:S(2)}, u32[]{:S(2)}) %collective-permute-start) | collective-permute-done | bytes 1048608 | tf_op jit(solution)/shard_map/while/body/eval_jaxpr/ppermute | solution.py:17
  525.2 1.8 bitcast_select_fusion.2
  527.1 3.0 multiply_convert_fusion.6
  530.1 2.2 fusion.92
  532.3 2.3 fusion.91
  535.2 1.5 copy.80
  538.0 2.3 copy.78
  540.2 3.8 fusion.93
  544.0 3.1 fusion.94
  547.2 1.3 convert_reduce_fusion.5
  550.9 22.6 %fusion.96 = bf16[512,4096]{1,0:T(8,128)(2,1)S(1)} fusion(bf16[512,1024]{1,0:T(8,128)(2,1)S(1)} %multiply_convert_fusion.7, bf16[1,1024,4096]{2,1,0:T(8,128)(2,1)S(1)} %bitcast.137), kind=kOutput, calls=%fused_computation.7.clone.1 | convolution fusion | flops 4431282176 | bytes 13631488 | tf_op jit(solution)/shard_map/while/body/eval_jaxpr/dot_general | solution.py:86
  573.5 4.9 convert_reduce_fusion.6
  579.8 4.4 collective-permute-start
  584.9 18.9 %collective-permute-done = bf16[512,1024]{1,0:T(8,128)(2,1)S(1)} collective-permute-done((bf16[512,1024]{1,0:T(8,128)(2,1)S(1)}, bf16[512,1024]{1,0:T(8,128)(2,1)S(1)}, u32[]{:S(2)}, u32[]{:S(2)}) %collective-permute-start) | collective-permute-done | bytes 1048608 | tf_op jit(solution)/shard_map/while/body/eval_jaxpr/ppermute | solution.py:17
  605.9 4.0 all-to-all-start
  609.9 5.3 all-to-all-done
  615.2 13.3 %all-gather = bf16[16,1,4,1,64]{4,2,3,1,0:T(4,128)(2,1)S(1)} all-gather(bf16[4,1,4,1,64]{4,2,3,1,0:T(4,128)(2,1)S(1)} %bitcast_bitcast_fusion), channel_id=2, replica_groups=mesh['dp'=8,'pipe'=4,'tensor'=4] {'pipe'}, dimensions={0}, use_global_device_ids=true | all-gather | bytes 10240 | tf_op jit(solution)/shard_map/all_gather | solution.py:21
  629.2 4.3 all-to-all-start.1
  633.5 5.3 all-to-all-done.1
  639.5 4.4 all-to-all-start.2
  643.9 7.6 %all-to-all-done.2 = f32[16,2,16]{2,1,0:T(2,128)S(1)} async-done(((f32[16,2,16]{2,1,0:T(2,128)}), f32[16,2,16]{2,1,0:T(2,128)S(1)}, u32[]{:S(2)}, u32[]{:S(2)}) %all-to-all-start.2) | async-done | bytes 2080 | tf_op jit(solution)/shard_map/all_to_all | solution.py:32
  (187 shorter events, 29.2 us)
Async XLA Ops:
  7.2 36.0 %all-gather.8.cloned.1.call-start = ((), (), s32[]{:S(2)}) async-start(), calls=%async_computation.4 | async-start | bytes 2621440 | tf_op jit(solution)/shard_map/all_gather | solution.py:122
  7.9 106.1 %all-gather.6.cloned.1.call-start = ((), (), s32[]{:S(2)}) async-start(), calls=%async_computation.3 | async-start | bytes 7864320 | tf_op jit(solution)/shard_map/all_gather | solution.py:121
  8.6 190.9 %all-gather.10.cloned.1.call-start = ((), (), s32[]{:S(2)}) async-start(), calls=%async_computation.5 | async-start | bytes 10485760 | tf_op jit(solution)/shard_map/all_gather | solution.py:123
  9.4 275.8 %all-gather.12.cloned.1.call-start = ((), (), s32[]{:S(2)}) async-start(), calls=%async_computation.6 | async-start | bytes 10485760 | tf_op jit(solution)/shard_map/all_gather | solution.py:124
  285.3 358.6 %copy-start.6 = (s32[1,2]{1,0:T(1,128)S(1)}, s32[1,2]{1,0:T(1,128)}, u32[]{:S(2)}) copy-start(s32[1,2]{1,0:T(1,128)} %param.17) | copy-start | bytes 28
  285.3 4.9 slice-start.4
  287.2 3.0 slice-start.5
  300.3 3.8 copy-start
  304.1 3.2 copy-start.5
  307.3 2.2 copy-start.2
  307.3 2.6 slice-start
  308.6 2.4 slice-start.1
  309.0 24.7 %slice-start.2 = ((s8[8388608]{0:T(1024)(128)(4,1)}), s8[4194304]{0:T(1024)(128)(4,1)S(1)}, s32[]{:S(2)}) async-start(s8[8388608]{0:T(1024)(128)(4,1)} %bitcast.138), calls=%async_computation.9 | async-start | bytes 8388608 | tf_op jit(solution)/shard_map/while
  311.0 22.6 %slice-start.3 = ((s8[8388608]{0:T(1024)(128)(4,1)}), s8[4194304]{0:T(1024)(128)(4,1)S(1)}, s32[]{:S(2)}) async-start(s8[8388608]{0:T(1024)(128)(4,1)} %bitcast.138), calls=%async_computation.10 | async-start | bytes 8388608 | tf_op jit(solution)/shard_map/while
  333.6 5.7 copy-start.1
  339.9 25.6 %collective-permute-start = (bf16[512,1024]{1,0:T(8,128)(2,1)S(1)}, bf16[512,1024]{1,0:T(8,128)(2,1)S(1)}, u32[]{:S(2)}, u32[]{:S(2)}) collective-permute-start(bf16[512,1024]{1,0:T(8,128)(2,1)S(1)} %get-tuple-element.564), channel_id=1, source_target_pairs={{0,4},{4,8},{8,12},{1,5},{5,9},{9,13},{2,6},{6,10},{10,14},{3,7},{... | collective-permute-start | bytes 3145736 | tf_op jit(solution)/shard_map/while/body/eval_jaxpr/ppermute | solution.py:17
  365.5 4.8 slice-start.4
  367.3 3.0 slice-start.5
  380.5 3.8 copy-start
  384.3 3.2 copy-start.5
  387.4 2.2 copy-start.2
  387.4 2.6 slice-start
  388.8 2.4 slice-start.1
  389.1 24.7 %slice-start.2 = ((s8[8388608]{0:T(1024)(128)(4,1)}), s8[4194304]{0:T(1024)(128)(4,1)S(1)}, s32[]{:S(2)}) async-start(s8[8388608]{0:T(1024)(128)(4,1)} %bitcast.138), calls=%async_computation.9 | async-start | bytes 8388608 | tf_op jit(solution)/shard_map/while
  391.2 22.6 %slice-start.3 = ((s8[8388608]{0:T(1024)(128)(4,1)}), s8[4194304]{0:T(1024)(128)(4,1)S(1)}, s32[]{:S(2)}) async-start(s8[8388608]{0:T(1024)(128)(4,1)} %bitcast.138), calls=%async_computation.10 | async-start | bytes 8388608 | tf_op jit(solution)/shard_map/while
  413.8 5.7 copy-start.1
  420.0 25.8 %collective-permute-start = (bf16[512,1024]{1,0:T(8,128)(2,1)S(1)}, bf16[512,1024]{1,0:T(8,128)(2,1)S(1)}, u32[]{:S(2)}, u32[]{:S(2)}) collective-permute-start(bf16[512,1024]{1,0:T(8,128)(2,1)S(1)} %get-tuple-element.564), channel_id=1, source_target_pairs={{0,4},{4,8},{8,12},{1,5},{5,9},{9,13},{2,6},{6,10},{10,14},{3,7},{... | collective-permute-start | bytes 3145736 | tf_op jit(solution)/shard_map/while/body/eval_jaxpr/ppermute | solution.py:17
  445.8 4.8 slice-start.4
  447.6 3.0 slice-start.5
  460.8 3.8 copy-start
  464.6 3.2 copy-start.5
  467.7 2.2 copy-start.2
  467.7 2.6 slice-start
  469.1 2.4 slice-start.1
  469.4 24.7 %slice-start.2 = ((s8[8388608]{0:T(1024)(128)(4,1)}), s8[4194304]{0:T(1024)(128)(4,1)S(1)}, s32[]{:S(2)}) async-start(s8[8388608]{0:T(1024)(128)(4,1)} %bitcast.138), calls=%async_computation.9 | async-start | bytes 8388608 | tf_op jit(solution)/shard_map/while
  471.5 22.6 %slice-start.3 = ((s8[8388608]{0:T(1024)(128)(4,1)}), s8[4194304]{0:T(1024)(128)(4,1)S(1)}, s32[]{:S(2)}) async-start(s8[8388608]{0:T(1024)(128)(4,1)} %bitcast.138), calls=%async_computation.10 | async-start | bytes 8388608 | tf_op jit(solution)/shard_map/while
  494.1 5.7 copy-start.1
  500.3 24.9 %collective-permute-start = (bf16[512,1024]{1,0:T(8,128)(2,1)S(1)}, bf16[512,1024]{1,0:T(8,128)(2,1)S(1)}, u32[]{:S(2)}, u32[]{:S(2)}) collective-permute-start(bf16[512,1024]{1,0:T(8,128)(2,1)S(1)} %get-tuple-element.564), channel_id=1, source_target_pairs={{0,4},{4,8},{8,12},{1,5},{5,9},{9,13},{2,6},{6,10},{10,14},{3,7},{... | collective-permute-start | bytes 3145736 | tf_op jit(solution)/shard_map/while/body/eval_jaxpr/ppermute | solution.py:17
  525.2 4.8 slice-start.4
  527.1 3.0 slice-start.5
  540.2 3.8 copy-start
  544.0 3.2 copy-start.5
  547.2 2.2 copy-start.2
  547.2 2.6 slice-start
  548.5 2.4 slice-start.1
  548.8 24.7 %slice-start.2 = ((s8[8388608]{0:T(1024)(128)(4,1)}), s8[4194304]{0:T(1024)(128)(4,1)S(1)}, s32[]{:S(2)}) async-start(s8[8388608]{0:T(1024)(128)(4,1)} %bitcast.138), calls=%async_computation.9 | async-start | bytes 8388608 | tf_op jit(solution)/shard_map/while
  550.9 22.6 %slice-start.3 = ((s8[8388608]{0:T(1024)(128)(4,1)}), s8[4194304]{0:T(1024)(128)(4,1)S(1)}, s32[]{:S(2)}) async-start(s8[8388608]{0:T(1024)(128)(4,1)} %bitcast.138), calls=%async_computation.10 | async-start | bytes 8388608 | tf_op jit(solution)/shard_map/while
  573.5 5.7 copy-start.1
  579.8 24.1 %collective-permute-start = (bf16[512,1024]{1,0:T(8,128)(2,1)S(1)}, bf16[512,1024]{1,0:T(8,128)(2,1)S(1)}, u32[]{:S(2)}, u32[]{:S(2)}) collective-permute-start(bf16[512,1024]{1,0:T(8,128)(2,1)S(1)} %get-tuple-element.564), channel_id=1, source_target_pairs={{0,4},{4,8},{8,12},{1,5},{5,9},{9,13},{2,6},{6,10},{10,14},{3,7},{... | collective-permute-start | bytes 3145736 | tf_op jit(solution)/shard_map/while/body/eval_jaxpr/ppermute | solution.py:17
  605.9 9.3 %all-to-all-start = ((bf16[4,2,128]{2,1,0:T(2,128)(2,1)}), bf16[4,2,128]{2,1,0:T(2,128)(2,1)S(1)}, u32[]{:S(2)}, u32[]{:S(2)}) async-start(bf16[4,2,128]{2,1,0:T(2,128)(2,1)} %reshape.179), calls=%async_computation | async-start | bytes 4096 | tf_op jit(solution)/shard_map/all_to_all | solution.py:169
  628.6 23.7 %copy-start.3 = (bf16[2,64]{1,0:T(2,128)(2,1)}, bf16[2,64]{1,0:T(2,128)(2,1)S(1)}, u32[]{:S(2)}) copy-start(bf16[2,64]{1,0:T(2,128)(2,1)S(1)} %get-tuple-element.459) | copy-start | bytes 772
  628.6 23.7 %copy-start.4 = (bf16[2,64]{1,0:T(2,128)(2,1)}, bf16[2,64]{1,0:T(2,128)(2,1)S(1)}, u32[]{:S(2)}) copy-start(bf16[2,64]{1,0:T(2,128)(2,1)S(1)} %get-tuple-element.460) | copy-start | bytes 772
  629.2 9.6 %all-to-all-start.1 = ((bf16[8,2,64]{2,1,0:T(2,128)(2,1)}), bf16[8,2,64]{2,1,0:T(2,128)(2,1)S(1)}, u32[]{:S(2)}, u32[]{:S(2)}) async-start(bf16[8,2,64]{2,1,0:T(2,128)(2,1)} %broadcast_in_dim.139), calls=%async_computation.1 | async-start | bytes 8192 | tf_op jit(solution)/shard_map/all_to_all | solution.py:32
  639.5 12.0 %all-to-all-start.2 = ((f32[16,2,16]{2,1,0:T(2,128)}), f32[16,2,16]{2,1,0:T(2,128)S(1)}, u32[]{:S(2)}, u32[]{:S(2)}) async-start(f32[16,2,16]{2,1,0:T(2,128)} %broadcast_in_dim.140), calls=%async_computation.2 | async-start | bytes 32768 | tf_op jit(solution)/shard_map/all_to_all | solution.py:32
Sparse Core Ops, SparseCore 0:
  9.6 33.4 all-gather.7
  44.8 69.1 all-gather.5
  115.7 83.7 all-gather.9
  201.0 84.0 all-gather.11
where the time goes:
time: 659 us
  waiting for transfers between devices  376 us (57%)
  matrix products  173 us (26%)
  starting transfers between devices  29.6 us (4%)
  local copies, waits for them, and re-layouts  26.4 us (4%)
  other arithmetic  22.3 us (3%)
  between operations  14.6 us (2%)
  blocking collectives  13.3 us (2%)
    dot_general x4, matrix products, encode_layer(): upward = jnp.dot(mixed, w_up, preferred_element_type=jnp.float32)  90.3 us
    all_gather x1, waiting for transfers between devices, per_device(): lax.all_gather(w_down, 'tensor', axis=1, tiled=True)  85.6 us
    all_gather x1, waiting for transfers between devices, per_device(): lax.all_gather(w_up, 'tensor', axis=2, tiled=True)  85.5 us
    ppermute x4, waiting for transfers between devices, from_behind(): lax.ppermute(value, axis, [(source, source + steps) for source in range(i...  80.8 us
    all_gather x1, waiting for transfers between devices, per_device(): lax.all_gather(w_qkv, 'tensor', axis=3, tiled=True)  70.9 us
    all_gather x1, waiting for transfers between devices, per_device(): lax.all_gather(w_out, 'tensor', axis=1, tiled=True)  32.4 us
    dot_general x8, matrix products, local_reduce(): jnp.einsum('sgk,gkd->gsd', left_parts, right_parts, preferred_element_typ...  24.7 us
    ppermute x4, starting transfers between devices, from_behind(): lax.ppermute(value, axis, [(source, source + steps) for source in range(i...  16.8 us
  transfers between devices with their start and end apart: 11, of which 11 were waited for; matrix products, arithmetic and copies ran while one was open for 0% of the time, Pallas kernels for 0%

commit v1 on v0

--- a/solution.py
+++ b/solution.py
@@ -9,6 +9,19 @@
 SOFTMAX_TEMPER = 0.05
 EPSILON = 1e-06
 LAYER_EPSILON = 1e-12
+
+
+def gather_around(x, axis, dim):
+    ways = lax.axis_size(axis)
+    up = [(d, (d + 1) % ways) for d in range(ways)]
+    down = [(d, (d - 1) % ways) for d in range(ways)]
+    earlier, later = ([x], [x])
+    for _ in range(ways // 2):
+        earlier.append(lax.ppermute(earlier[-1], axis, up))
+    for _ in range((ways - 1) // 2):
+        later.append(lax.ppermute(later[-1], axis, down))
+    line = jnp.concatenate([*earlier[::-1], *later[1:]], axis=dim)
+    return jnp.roll(line, (lax.axis_index(axis) - ways // 2) * x.shape[dim], axis=dim)
 
 
 def from_behind(value, axis, steps):
@@ -121,7 +134,7 @@
         lax.all_gather(w_qkv, "tensor", axis=3, tiled=True),
         lax.all_gather(w_out, "tensor", axis=1, tiled=True),
         lax.all_gather(w_up, "tensor", axis=2, tiled=True),
-        lax.all_gather(w_down, "tensor", axis=1, tiled=True),
+        gather_around(w_down, "tensor", 1),
     )
     share = seq_count // tensor_count
     first_seq = lax.axis_index("tensor") * share

time: 659 us -> 631 us (0.958)
  waiting for transfers between devices: 376 us -> 313 us
  local copies, waits for them, and re-layouts: 26.4 us -> 56.1 us
    ppermute x0 -> x3, waiting for transfers between devices: none -> 151 us  [the longest x2 151 us: gather_around(): earlier.append(lax.ppermute(earlier[-1], axis, up))]
    all_gather x1 -> x0, waiting for transfers between devices: 85.6 us -> none  [per_device(): lax.all_gather(w_down, 'tensor', axis=1, tiled=True)]
    all_gather x1, waiting for transfers between devices: 70.9 us -> 0.01 us  [per_device(): lax.all_gather(w_qkv, 'tensor', axis=3, tiled=True)]
    all_gather x1, waiting for transfers between devices: 32.4 us -> 0.01 us  [per_device(): lax.all_gather(w_out, 'tensor', axis=1, tiled=True)]
    all_gather x1, waiting for transfers between devices: 85.5 us -> 61.1 us  [per_device(): lax.all_gather(w_up, 'tensor', axis=2, tiled=True)]
    unnamed x9 -> x22, local copies, waits for them, and re-layouts: 0.76 us -> 19.3 us
    dynamic_slice x0 -> x1, local copies, waits for them, and re-layouts: none -> 7.86 us  [gather_around(): jnp.roll(line, (lax.axis_index(axis) - ways // 2) * x.shape[dim], axis=dim)]
  transfers between devices with their start and end apart: 11 -> 13, of which waited for: 11 -> 10; matrix products, arithmetic and copies ran while one was open for 0% -> 5% of each run, Pallas kernels for 0% -> 0%
where the time goes in v1:
time: 631 us
  waiting for transfers between devices  313 us (50%)
  matrix products  173 us (27%)
  local copies, waits for them, and re-layouts  56.1 us (9%)
  starting transfers between devices  35 us (6%)
  other arithmetic  22 us (3%)
  between operations  14.6 us (2%)
  blocking collectives  13.3 us (2%)
    ppermute x2, waiting for transfers between devices, gather_around(): earlier.append(lax.ppermute(earlier[-1], axis, up))  151 us
    dot_general x4, matrix products, encode_layer(): upward = jnp.dot(mixed, w_up, preferred_element_type=jnp.float32)  90.3 us
    ppermute x4, waiting for transfers between devices, from_behind(): lax.ppermute(value, axis, [(source, source + steps) for source in range(i...  81 us
    all_gather x1, waiting for transfers between devices, per_device(): lax.all_gather(w_up, 'tensor', axis=2, tiled=True)  61.1 us
    dot_general x8, matrix products, local_reduce(): jnp.einsum('sgk,gkd->gsd', left_parts, right_parts, preferred_element_typ...  24.7 us
    unnamed x22, local copies, waits for them, and re-layouts  19.3 us
    ppermute x4, starting transfers between devices, from_behind(): lax.ppermute(value, axis, [(source, source + steps) for source in range(i...  16.8 us
    dot_general x4, matrix products, encode_layer(): jnp.einsum('qhe,khe->hqk', query_heads, key_heads, preferred_element_type...  15.1 us
  transfers between devices with their start and end apart: 13, of which 10 were waited for; matrix products, arithmetic and copies ran while one was open for 5% of the time, Pallas kernels for 0%

profile of v1, /device:TPU:0, one launch (start us, length us, event | category | flops | bytes accessed | tf_op | source)
XLA Modules:
  0.0 630.6 jit_solution(7756604383222901046)
XLA Ops:
  9.4 2.1 collective-permute-start.1
  11.5 66.2 %collective-permute-done.1 = bf16[1,1024,1024]{2,1,0:T(8,128)(2,1)} collective-permute-done((bf16[1,1024,1024]{2,1,0:T(8,128)(2,1)}, bf16[1,1024,1024]{2,1,0:T(8,128)(2,1)}, u32[]{:S(2)}, u32[]{:S(2)}) %collective-permute-start.1) | collective-permute-done | bytes 2097184 | tf_op jit(solution)/shard_map/ppermute | solution.py:20
  78.5 2.5 collective-permute-start.3
  81.8 84.6 %collective-permute-done.2 = bf16[1,1024,1024]{2,1,0:T(8,128)(2,1)} collective-permute-done((bf16[1,1024,1024]{2,1,0:T(8,128)(2,1)}, bf16[1,1024,1024]{2,1,0:T(8,128)(2,1)}, u32[]{:S(2)}, u32[]{:S(2)}) %collective-permute-start.2) | collective-permute-done | bytes 2097184 | tf_op jit(solution)/shard_map/ppermute | solution.py:20
  166.4 3.1 constant_dynamic-update-slice_fusion.7
  169.5 3.1 constant_dynamic-update-slice_fusion.6
  174.1 3.1 constant_dynamic-update-slice_fusion.4
  177.2 3.1 constant_dynamic-update-slice_fusion.3
  180.3 3.1 constant_dynamic-update-slice_fusion.2
  184.9 3.3 constant_dynamic-update-slice_fusion
  188.2 7.9 %constant_dynamic-slice_fusion.1 = bf16[1,4096,1024]{2,1,0:T(8,128)(2,1)} fusion(bf16[1,8192,1024]{2,1,0:T(8,128)(2,1)} %constant_dynamic-update-slice_fusion, s32[]{:T(128)S(6)} %select_n.125), kind=kLoop, calls=%fused_computation.83 | loop fusion | bytes 16777220 | tf_op jit(solution)/shard_map/jit(_roll_dynamic)/dynamic_slice | solution.py:24
  196.1 61.1 %all-gather.9.cloned.1.call-done = bf16[1,1024,4096]{2,1,0:T(8,128)(2,1)} async-done(((bf16[1,1024,1024]{2,1,0:T(8,128)(2,1)}), bf16[1,1024,4096]{2,1,0:T(8,128)(2,1)}) %all-gather.9.cloned.1.call-update) | async-done | bytes 8388624 | tf_op jit(solution)/shard_map/all_gather | solution.py:136
  257.3 318.3 %while.18 = (s32[]{:T(128)}, bf16[512,1024]{1,0:T(8,128)(2,1)S(1)}, f32[1,1024]{1,0:T(1,128)S(1)}, pred[]{:T(512)}, s32[]{:T(128)}, /*index=5*/bf16[2,512,1024]{...) while((s32[]{:T(128)}, bf16[512,1024]{1,0:T(8,128)(2,1)S(1)}, ...), condition=%wide.region_9.10_spmd.clone, body=%wide.region_0.9_spmd.clone.sunk | while | flops 14147382272 | bytes 201464576 | solution.py:177
  257.5 1.8 bitcast_select_fusion.2
  259.4 3.0 multiply_convert_fusion.6
  262.4 2.3 fusion.92
  264.7 2.3 fusion.91
  270.2 2.3 copy.78
  272.5 3.8 fusion.93
  276.3 3.1 fusion.94
  283.1 22.6 %fusion.96 = bf16[512,4096]{1,0:T(8,128)(2,1)S(1)} fusion(bf16[512,1024]{1,0:T(8,128)(2,1)S(1)} %multiply_convert_fusion.7, bf16[1,1024,4096]{2,1,0:T(8,128)(2,1)S(1)} %bitcast.140), kind=kOutput, calls=%fused_computation.7.clone.1 | convolution fusion | flops 4431282176 | bytes 13631488 | tf_op jit(solution)/shard_map/while/body/eval_jaxpr/dot_general | solution.py:99
  305.7 4.9 convert_reduce_fusion.6
  312.0 3.4 collective-permute-start
  316.0 21.5 %collective-permute-done = bf16[512,1024]{1,0:T(8,128)(2,1)S(1)} collective-permute-done((bf16[512,1024]{1,0:T(8,128)(2,1)S(1)}, bf16[512,1024]{1,0:T(8,128)(2,1)S(1)}, u32[]{:S(2)}, u32[]{:S(2)}) %collective-permute-start) | collective-permute-done | bytes 1048608 | tf_op jit(solution)/shard_map/while/body/eval_jaxpr/ppermute | solution.py:30
  337.6 1.8 bitcast_select_fusion.2
  339.4 3.0 multiply_convert_fusion.6
  342.4 2.3 fusion.92
  344.8 2.3 fusion.91
  350.2 2.3 copy.78
  352.5 3.8 fusion.93
  356.3 3.1 fusion.94
  363.2 22.6 %fusion.96 = bf16[512,4096]{1,0:T(8,128)(2,1)S(1)} fusion(bf16[512,1024]{1,0:T(8,128)(2,1)S(1)} %multiply_convert_fusion.7, bf16[1,1024,4096]{2,1,0:T(8,128)(2,1)S(1)} %bitcast.140), kind=kOutput, calls=%fused_computation.7.clone.1 | convolution fusion | flops 4431282176 | bytes 13631488 | tf_op jit(solution)/shard_map/while/body/eval_jaxpr/dot_general | solution.py:99
  385.8 4.9 convert_reduce_fusion.6
  392.0 4.5 collective-permute-start
  397.1 20.7 %collective-permute-done = bf16[512,1024]{1,0:T(8,128)(2,1)S(1)} collective-permute-done((bf16[512,1024]{1,0:T(8,128)(2,1)S(1)}, bf16[512,1024]{1,0:T(8,128)(2,1)S(1)}, u32[]{:S(2)}, u32[]{:S(2)}) %collective-permute-start) | collective-permute-done | bytes 1048608 | tf_op jit(solution)/shard_map/while/body/eval_jaxpr/ppermute | solution.py:30
  417.8 1.8 bitcast_select_fusion.2
  419.6 3.0 multiply_convert_fusion.6
  422.7 2.3 fusion.92
  425.0 2.3 fusion.91
  430.4 2.3 copy.78
  432.7 3.8 fusion.93
  436.5 3.1 fusion.94
  443.4 22.6 %fusion.96 = bf16[512,4096]{1,0:T(8,128)(2,1)S(1)} fusion(bf16[512,1024]{1,0:T(8,128)(2,1)S(1)} %multiply_convert_fusion.7, bf16[1,1024,4096]{2,1,0:T(8,128)(2,1)S(1)} %bitcast.140), kind=kOutput, calls=%fused_computation.7.clone.1 | convolution fusion | flops 4431282176 | bytes 13631488 | tf_op jit(solution)/shard_map/while/body/eval_jaxpr/dot_general | solution.py:99
  466.0 4.9 convert_reduce_fusion.6
  472.2 4.5 collective-permute-start
  477.3 19.8 %collective-permute-done = bf16[512,1024]{1,0:T(8,128)(2,1)S(1)} collective-permute-done((bf16[512,1024]{1,0:T(8,128)(2,1)S(1)}, bf16[512,1024]{1,0:T(8,128)(2,1)S(1)}, u32[]{:S(2)}, u32[]{:S(2)}) %collective-permute-start) | collective-permute-done | bytes 1048608 | tf_op jit(solution)/shard_map/while/body/eval_jaxpr/ppermute | solution.py:30
  497.1 1.8 bitcast_select_fusion.2
  499.0 3.0 multiply_convert_fusion.6
  502.0 2.3 fusion.92
  504.3 2.3 fusion.91
  509.8 2.3 copy.78
  512.1 3.8 fusion.93
  515.9 3.1 fusion.94
  522.8 22.6 %fusion.96 = bf16[512,4096]{1,0:T(8,128)(2,1)S(1)} fusion(bf16[512,1024]{1,0:T(8,128)(2,1)S(1)} %multiply_convert_fusion.7, bf16[1,1024,4096]{2,1,0:T(8,128)(2,1)S(1)} %bitcast.140), kind=kOutput, calls=%fused_computation.7.clone.1 | convolution fusion | flops 4431282176 | bytes 13631488 | tf_op jit(solution)/shard_map/while/body/eval_jaxpr/dot_general | solution.py:99
  545.4 4.9 convert_reduce_fusion.6
  551.6 4.5 collective-permute-start
  556.7 19.0 %collective-permute-done = bf16[512,1024]{1,0:T(8,128)(2,1)S(1)} collective-permute-done((bf16[512,1024]{1,0:T(8,128)(2,1)S(1)}, bf16[512,1024]{1,0:T(8,128)(2,1)S(1)}, u32[]{:S(2)}, u32[]{:S(2)}) %collective-permute-start) | collective-permute-done | bytes 1048608 | tf_op jit(solution)/shard_map/while/body/eval_jaxpr/ppermute | solution.py:30
  577.7 4.0 all-to-all-start
  581.7 5.3 all-to-all-done
  587.1 13.3 %all-gather = bf16[16,1,4,1,64]{4,2,3,1,0:T(4,128)(2,1)S(1)} all-gather(bf16[4,1,4,1,64]{4,2,3,1,0:T(4,128)(2,1)S(1)} %bitcast_bitcast_fusion), channel_id=2, replica_groups=mesh['dp'=8,'pipe'=4,'tensor'=4] {'pipe'}, dimensions={0}, use_global_device_ids=true | all-gather | bytes 10240 | tf_op jit(solution)/shard_map/all_gather | solution.py:34
  601.1 4.3 all-to-all-start.1
  605.4 5.3 all-to-all-done.1
  611.4 4.4 all-to-all-start.2
  615.8 7.6 %all-to-all-done.2 = f32[16,2,16]{2,1,0:T(2,128)S(1)} async-done(((f32[16,2,16]{2,1,0:T(2,128)}), f32[16,2,16]{2,1,0:T(2,128)S(1)}, u32[]{:S(2)}, u32[]{:S(2)}) %all-to-all-start.2) | async-done | bytes 2080 | tf_op jit(solution)/shard_map/all_to_all | solution.py:45
  (189 shorter events, 43.3 us)
Async XLA Ops:
  7.2 165.4 %copy-start.1 = (bf16[1,1024,1024]{2,1,0:T(8,128)(2,1)S(1)}, bf16[1,1024,1024]{2,1,0:T(8,128)(2,1)}, u32[]{:S(2)}) copy-start(bf16[1,1024,1024]{2,1,0:T(8,128)(2,1)} %param.21) | copy-start | bytes 6291460
  7.2 188.9 %all-gather.7.cloned.1.call-start = ((), (), s32[]{:S(2)}) async-start(), calls=%async_computation.4 | async-start | bytes 2621440 | tf_op jit(solution)/shard_map/all_gather | solution.py:135
  7.9 188.2 %all-gather.5.cloned.1.call-start = ((), (), s32[]{:S(2)}) async-start(), calls=%async_computation.3 | async-start | bytes 7864320 | tf_op jit(solution)/shard_map/all_gather | solution.py:134
  8.7 248.5 %all-gather.9.cloned.1.call-start = ((), (), s32[]{:S(2)}) async-start(), calls=%async_computation.5 | async-start | bytes 10485760 | tf_op jit(solution)/shard_map/all_gather | solution.py:136
  9.4 68.3 %collective-permute-start.1 = (bf16[1,1024,1024]{2,1,0:T(8,128)(2,1)}, bf16[1,1024,1024]{2,1,0:T(8,128)(2,1)}, u32[]{:S(2)}, u32[]{:S(2)}) collective-permute-start(bf16[1,1024,1024]{2,1,0:T(8,128)(2,1)} %param.21), channel_id=1, source_target_pairs={{0,1},{1,2},{2,3},{3,0},{4,5},{5,6},{6,7},{7,4},{8,9},{9,10},{10,1... | collective-permute-start | bytes 6291464 | tf_op jit(solution)/shard_map/ppermute | solution.py:20
  77.7 88.8 %collective-permute-start.2 = (bf16[1,1024,1024]{2,1,0:T(8,128)(2,1)}, bf16[1,1024,1024]{2,1,0:T(8,128)(2,1)}, u32[]{:S(2)}, u32[]{:S(2)}) collective-permute-start(bf16[1,1024,1024]{2,1,0:T(8,128)(2,1)} %collective-permute-done.1), channel_id=1, source_target_pairs={{0,1},{1,2},{2,3},{3,0},{4,5},{5,6},{6,7},{7,4},{8,9},{9,10},{10,1... | collective-permute-start | bytes 6291464 | tf_op jit(solution)/shard_map/ppermute | solution.py:20
  78.5 95.6 %collective-permute-start.3 = (bf16[1,1024,1024]{2,1,0:T(8,128)(2,1)}, bf16[1,1024,1024]{2,1,0:T(8,128)(2,1)}, u32[]{:S(2)}, u32[]{:S(2)}) collective-permute-start(bf16[1,1024,1024]{2,1,0:T(8,128)(2,1)} %param.21), channel_id=1, source_target_pairs={{0,3},{1,0},{2,1},{3,2},{4,7},{5,4},{6,5},{7,6},{8,11},{9,8},{10,9... | collective-permute-start | bytes 6291464 | tf_op jit(solution)/shard_map/ppermute | solution.py:22
  188.2 69.1 %copy-start.2 = (f32[1,1024]{1,0:T(1,128)S(1)}, f32[1,1024]{1,0:T(1,128)}, u32[]{:S(2)}) copy-start(f32[1,1024]{1,0:T(1,128)} %param.23) | copy-start | bytes 12292
  188.2 69.1 %copy-start.3 = (f32[1,1024]{1,0:T(1,128)S(1)}, f32[1,1024]{1,0:T(1,128)}, u32[]{:S(2)}) copy-start(f32[1,1024]{1,0:T(1,128)} %param.22) | copy-start | bytes 12292
  257.3 358.5 %copy-start.7 = (s32[1,2]{1,0:T(1,128)S(1)}, s32[1,2]{1,0:T(1,128)}, u32[]{:S(2)}) copy-start(s32[1,2]{1,0:T(1,128)} %param.17) | copy-start | bytes 28
  257.5 4.9 slice-start.4
  259.4 3.0 slice-start.5
  272.5 3.8 copy-start
  276.3 3.2 copy-start.6
  279.4 2.6 slice-start.2
  280.7 2.4 slice-start.3
  281.1 24.7 %slice-start = ((s8[8388608]{0:T(1024)(128)(4,1)}), s8[4194304]{0:T(1024)(128)(4,1)S(1)}, s32[]{:S(2)}) async-start(s8[8388608]{0:T(1024)(128)(4,1)} %bitcast.130), calls=%async_computation.6 | async-start | bytes 8388608 | tf_op jit(solution)/shard_map/while
  283.1 22.6 %slice-start.1 = ((s8[8388608]{0:T(1024)(128)(4,1)}), s8[4194304]{0:T(1024)(128)(4,1)S(1)}, s32[]{:S(2)}) async-start(s8[8388608]{0:T(1024)(128)(4,1)} %bitcast.130), calls=%async_computation.7 | async-start | bytes 8388608 | tf_op jit(solution)/shard_map/while
  312.0 25.6 %collective-permute-start = (bf16[512,1024]{1,0:T(8,128)(2,1)S(1)}, bf16[512,1024]{1,0:T(8,128)(2,1)S(1)}, u32[]{:S(2)}, u32[]{:S(2)}) collective-permute-start(bf16[512,1024]{1,0:T(8,128)(2,1)S(1)} %get-tuple-element.564), channel_id=1, source_target_pairs={{0,4},{4,8},{8,12},{1,5},{5,9},{9,13},{2,6},{6,10},{10,14},{3,7},{... | collective-permute-start | bytes 3145736 | tf_op jit(solution)/shard_map/while/body/eval_jaxpr/ppermute | solution.py:30
  337.6 4.8 slice-start.4
  339.4 3.0 slice-start.5
  352.5 3.8 copy-start
  356.3 3.2 copy-start.6
  359.5 2.6 slice-start.2
  360.8 2.4 slice-start.3
  361.1 24.7 %slice-start = ((s8[8388608]{0:T(1024)(128)(4,1)}), s8[4194304]{0:T(1024)(128)(4,1)S(1)}, s32[]{:S(2)}) async-start(s8[8388608]{0:T(1024)(128)(4,1)} %bitcast.130), calls=%async_computation.6 | async-start | bytes 8388608 | tf_op jit(solution)/shard_map/while
  363.2 22.6 %slice-start.1 = ((s8[8388608]{0:T(1024)(128)(4,1)}), s8[4194304]{0:T(1024)(128)(4,1)S(1)}, s32[]{:S(2)}) async-start(s8[8388608]{0:T(1024)(128)(4,1)} %bitcast.130), calls=%async_computation.7 | async-start | bytes 8388608 | tf_op jit(solution)/shard_map/while
  392.0 25.8 %collective-permute-start = (bf16[512,1024]{1,0:T(8,128)(2,1)S(1)}, bf16[512,1024]{1,0:T(8,128)(2,1)S(1)}, u32[]{:S(2)}, u32[]{:S(2)}) collective-permute-start(bf16[512,1024]{1,0:T(8,128)(2,1)S(1)} %get-tuple-element.564), channel_id=1, source_target_pairs={{0,4},{4,8},{8,12},{1,5},{5,9},{9,13},{2,6},{6,10},{10,14},{3,7},{... | collective-permute-start | bytes 3145736 | tf_op jit(solution)/shard_map/while/body/eval_jaxpr/ppermute | solution.py:30
  417.8 4.8 slice-start.4
  419.6 3.0 slice-start.5
  432.7 3.8 copy-start
  436.5 3.2 copy-start.6
  439.7 2.6 slice-start.2
  441.0 2.4 slice-start.3
  441.3 24.7 %slice-start = ((s8[8388608]{0:T(1024)(128)(4,1)}), s8[4194304]{0:T(1024)(128)(4,1)S(1)}, s32[]{:S(2)}) async-start(s8[8388608]{0:T(1024)(128)(4,1)} %bitcast.130), calls=%async_computation.6 | async-start | bytes 8388608 | tf_op jit(solution)/shard_map/while
  443.4 22.6 %slice-start.1 = ((s8[8388608]{0:T(1024)(128)(4,1)}), s8[4194304]{0:T(1024)(128)(4,1)S(1)}, s32[]{:S(2)}) async-start(s8[8388608]{0:T(1024)(128)(4,1)} %bitcast.130), calls=%async_computation.7 | async-start | bytes 8388608 | tf_op jit(solution)/shard_map/while
  472.2 24.9 %collective-permute-start = (bf16[512,1024]{1,0:T(8,128)(2,1)S(1)}, bf16[512,1024]{1,0:T(8,128)(2,1)S(1)}, u32[]{:S(2)}, u32[]{:S(2)}) collective-permute-start(bf16[512,1024]{1,0:T(8,128)(2,1)S(1)} %get-tuple-element.564), channel_id=1, source_target_pairs={{0,4},{4,8},{8,12},{1,5},{5,9},{9,13},{2,6},{6,10},{10,14},{3,7},{... | collective-permute-start | bytes 3145736 | tf_op jit(solution)/shard_map/while/body/eval_jaxpr/ppermute | solution.py:30
  497.1 4.8 slice-start.4
  499.0 3.0 slice-start.5
  512.1 3.8 copy-start
  515.9 3.2 copy-start.6
  519.0 2.6 slice-start.2
  520.3 2.4 slice-start.3
  520.7 24.7 %slice-start = ((s8[8388608]{0:T(1024)(128)(4,1)}), s8[4194304]{0:T(1024)(128)(4,1)S(1)}, s32[]{:S(2)}) async-start(s8[8388608]{0:T(1024)(128)(4,1)} %bitcast.130), calls=%async_computation.6 | async-start | bytes 8388608 | tf_op jit(solution)/shard_map/while
  522.7 22.6 %slice-start.1 = ((s8[8388608]{0:T(1024)(128)(4,1)}), s8[4194304]{0:T(1024)(128)(4,1)S(1)}, s32[]{:S(2)}) async-start(s8[8388608]{0:T(1024)(128)(4,1)} %bitcast.130), calls=%async_computation.7 | async-start | bytes 8388608 | tf_op jit(solution)/shard_map/while
  551.6 24.0 %collective-permute-start = (bf16[512,1024]{1,0:T(8,128)(2,1)S(1)}, bf16[512,1024]{1,0:T(8,128)(2,1)S(1)}, u32[]{:S(2)}, u32[]{:S(2)}) collective-permute-start(bf16[512,1024]{1,0:T(8,128)(2,1)S(1)} %get-tuple-element.564), channel_id=1, source_target_pairs={{0,4},{4,8},{8,12},{1,5},{5,9},{9,13},{2,6},{6,10},{10,14},{3,7},{... | collective-permute-start | bytes 3145736 | tf_op jit(solution)/shard_map/while/body/eval_jaxpr/ppermute | solution.py:30
  577.7 9.3 %all-to-all-start = ((bf16[4,2,128]{2,1,0:T(2,128)(2,1)}), bf16[4,2,128]{2,1,0:T(2,128)(2,1)S(1)}, u32[]{:S(2)}, u32[]{:S(2)}) async-start(bf16[4,2,128]{2,1,0:T(2,128)(2,1)} %reshape.179), calls=%async_computation | async-start | bytes 4096 | tf_op jit(solution)/shard_map/all_to_all | solution.py:182
  600.5 23.6 %copy-start.4 = (bf16[2,64]{1,0:T(2,128)(2,1)}, bf16[2,64]{1,0:T(2,128)(2,1)S(1)}, u32[]{:S(2)}) copy-start(bf16[2,64]{1,0:T(2,128)(2,1)S(1)} %get-tuple-element.459) | copy-start | bytes 772
  600.5 23.6 %copy-start.5 = (bf16[2,64]{1,0:T(2,128)(2,1)}, bf16[2,64]{1,0:T(2,128)(2,1)S(1)}, u32[]{:S(2)}) copy-start(bf16[2,64]{1,0:T(2,128)(2,1)S(1)} %get-tuple-element.460) | copy-start | bytes 772
  601.1 9.6 %all-to-all-start.1 = ((bf16[8,2,64]{2,1,0:T(2,128)(2,1)}), bf16[8,2,64]{2,1,0:T(2,128)(2,1)S(1)}, u32[]{:S(2)}, u32[]{:S(2)}) async-start(bf16[8,2,64]{2,1,0:T(2,128)(2,1)} %broadcast_in_dim.139), calls=%async_computation.1 | async-start | bytes 8192 | tf_op jit(solution)/shard_map/all_to_all | solution.py:45
  611.4 12.0 %all-to-all-start.2 = ((f32[16,2,16]{2,1,0:T(2,128)}), f32[16,2,16]{2,1,0:T(2,128)S(1)}, u32[]{:S(2)}, u32[]{:S(2)}) async-start(f32[16,2,16]{2,1,0:T(2,128)} %broadcast_in_dim.140), calls=%async_computation.2 | async-start | bytes 32768 | tf_op jit(solution)/shard_map/all_to_all | solution.py:45
Sparse Core Ops, SparseCore 0:
  9.6 50.4 all-gather.6
  61.8 110.2 all-gather.4
  173.7 83.3 all-gather.8
